TPU v7x, 32 devices: a whole 2x2x4 slice. The times are simulated.
32 devices in a mesh: layer: 4 (over z), facet: 8 (over y, x, core).
Axes of the slice: x: 2, y: 2, z: 4, core: 2. Of those that a mesh axis runs over, the one named last changes fastest.
Arguments:
- model_strip: bfloat16 [8, 2, 64, 8192], P('facet', None, None, 'layer'), may hold values from -6 to 6
- screen_angle: bfloat16 [4, 8, 64, 8192], P('layer', 'facet'), may hold values from -3.140625 to 3.140625
- facet_window: float32 [8, 8192], P('facet'), may hold values from 0.04 to 0.16
- facet_shift: int32 [8], P('facet'), may hold values from 0 to 8191
- kernel_taps: float32 [7], replicated, may hold values from 0.2 to 0.6
- plane_angle: float32 [4, 8], P('layer'), may hold values from -3.140625 to 3.140625
- u_cell: int32 [4, 128, 512], P('layer', 'facet'), may hold values from 0 to 63
- v_cell: int32 [4, 128, 512], P('layer', 'facet'), may hold values from 0 to 63
- w_plane: int32 [4, 128, 512], P('layer', 'facet'), may hold values from 0 to 7
- observed: float32 [4, 128, 2, 512], P('layer', 'facet'), may hold values from -6 to 6
Outputs:
- residual: float32 [4, 128, 2, 512], P('layer', 'facet')
- gradient: float32 [8, 2, 64, 8192], P('facet', None, None, 'layer')
All inputs are finite; a program needn't handle non-finite values.
Results may differ from a plain program's by a relative error of at most 0.009.
Values may be sent and summed in bfloat16 or wider, within the bound.
A program may use at most 64 MiB of HBM per device.

v0:
```python
import math
import jax
import jax.numpy as jnp
from jax import lax
from jax.sharding import PartitionSpec as P

STRIP_LEN = 8192
SUB_ROWS = 64
STRIP_COLS = 64
PLANES = 8
SUBGRIDS = 128
back_gain = 8.0


def fourier_table(length):
    positions = jnp.arange(length, dtype=jnp.int32)
    turn_count = positions[:, None] * positions[None, :] % length
    angles = 2.0 * math.pi / length * turn_count.astype(jnp.float32)
    norm_scale = 1.0 / math.sqrt(length)
    return (jnp.stack([jnp.cos(angles), -jnp.sin(angles)]) * norm_scale).astype(jnp.bfloat16)


def twiddle():
    low_index = jnp.arange(SUB_ROWS, dtype=jnp.int32)
    high_index = jnp.arange(SUBGRIDS, dtype=jnp.int32)
    turn_count = low_index[:, None] * high_index[None, :] % STRIP_LEN
    angles = 2.0 * math.pi / STRIP_LEN * turn_count.astype(jnp.float32)
    return (jnp.cos(angles), -jnp.sin(angles))


def facet_factor(window, shift_cells):
    positions = jnp.arange(STRIP_LEN, dtype=jnp.int32)
    turn_count = positions * shift_cells % STRIP_LEN
    angles = 2.0 * math.pi / STRIP_LEN * turn_count.astype(jnp.float32)
    factor_real = (window * jnp.cos(angles)).reshape(SUBGRIDS, SUB_ROWS, 1)
    factor_imag = (-window * jnp.sin(angles)).reshape(SUBGRIDS, SUB_ROWS, 1)
    return (factor_real, factor_imag)


def forward(screened, window, shift_cells):
    grid_view = screened.reshape(2, STRIP_COLS, SUB_ROWS, SUBGRIDS)
    section_one = jnp.einsum(
        "tka,pcab->tpckb", fourier_table(SUB_ROWS), grid_view, preferred_element_type=jnp.float32
    )
    real_part = section_one[0, 0] - section_one[1, 1]
    imag_part = section_one[0, 1] + section_one[1, 0]
    twist_real, twist_imag = twiddle()
    mixed = jnp.stack(
        [
            real_part * twist_real - imag_part * twist_imag,
            real_part * twist_imag + imag_part * twist_real,
        ]
    ).astype(jnp.bfloat16)
    section_two = jnp.einsum(
        "tjb,pckb->tpjkc", fourier_table(SUBGRIDS), mixed, preferred_element_type=jnp.float32
    )
    spec_real = section_two[0, 0] - section_two[1, 1]
    spec_imag = section_two[0, 1] + section_two[1, 0]
    factor_real, factor_imag = facet_factor(window, shift_cells)
    return jnp.concatenate(
        [
            spec_real * factor_real - spec_imag * factor_imag,
            spec_real * factor_imag + spec_imag * factor_real,
        ],
        axis=2,
    ).astype(jnp.bfloat16)


def backward(all_grids, window, shift_cells, screen_phase):
    values = all_grids.astype(jnp.float32)
    grid_real = values[:, :, :STRIP_COLS]
    grid_imag = values[:, :, STRIP_COLS:]
    factor_real, factor_imag = facet_factor(window, shift_cells)
    spectral = jnp.stack(
        [
            grid_real * factor_real + grid_imag * factor_imag,
            grid_imag * factor_real - grid_real * factor_imag,
        ]
    ).astype(jnp.bfloat16)
    section_two = jnp.einsum(
        "tjb,pjkc->tpckb", fourier_table(SUBGRIDS), spectral, preferred_element_type=jnp.float32
    )
    half_real = section_two[0, 0] + section_two[1, 1]
    half_imag = section_two[0, 1] - section_two[1, 0]
    twist_real, twist_imag = twiddle()
    mixed = jnp.stack(
        [
            half_real * twist_real + half_imag * twist_imag,
            half_imag * twist_real - half_real * twist_imag,
        ]
    ).astype(jnp.bfloat16)
    section_one = jnp.einsum(
        "tka,pckb->tpcab", fourier_table(SUB_ROWS), mixed, preferred_element_type=jnp.float32
    )
    image_real = (section_one[0, 0] + section_one[1, 1]).reshape(STRIP_COLS, STRIP_LEN)
    image_imag = (section_one[0, 1] - section_one[1, 0]).reshape(STRIP_COLS, STRIP_LEN)
    phases = screen_phase.astype(jnp.float32)
    cosine = jnp.cos(phases)
    sine_part = jnp.sin(phases)
    return back_gain * jnp.stack(
        [image_real * cosine + image_imag * sine_part, image_imag * cosine - image_real * sine_part]
    )


def spread(cell_index, length, kernel_taps):
    tap_count = kernel_taps.shape[0]
    offset = (jnp.arange(length, dtype=jnp.int32)[None, :] - cell_index[:, None]) % length
    wanted = (jnp.arange(tap_count, dtype=jnp.int32) - tap_count // 2) % length
    matches = (offset[:, :, None] == wanted[None, None, :]).astype(jnp.float32)
    return jnp.sum(matches * kernel_taps, axis=2)


def adjoint_from(row_weights, column_weights, weighted):
    spread_cols = jnp.concatenate(
        [weighted[0][:, None] * column_weights, weighted[1][:, None] * column_weights], axis=1
    )
    return jnp.dot(row_weights.T, spread_cols, precision=lax.Precision.HIGHEST)


def degrid(subgrid, row_cells, column_cells, plane, observed_vis, angle_table, kernel_taps):
    row_weights = spread(row_cells, SUB_ROWS, kernel_taps)
    column_weights = spread(column_cells, STRIP_COLS, kernel_taps)
    kernel_rows = jnp.dot(row_weights, subgrid, precision=lax.Precision.HIGHEST)
    model_real = jnp.sum(kernel_rows[:, :STRIP_COLS] * column_weights, axis=1)
    model_imag = jnp.sum(kernel_rows[:, STRIP_COLS:] * column_weights, axis=1)
    plane_pick = (plane[:, None] == jnp.arange(PLANES, dtype=jnp.int32)[None, :]).astype(
        jnp.float32
    )
    phase_angle = jnp.sum(plane_pick * angle_table[None, :], axis=1)
    cosine = jnp.cos(phase_angle)
    sine_part = jnp.sin(phase_angle)
    residual_real = observed_vis[0] - (model_real * cosine - model_imag * sine_part)
    residual_imag = observed_vis[1] - (model_real * sine_part + model_imag * cosine)
    weighted = jnp.stack(
        [
            residual_real * cosine + residual_imag * sine_part,
            residual_imag * cosine - residual_real * sine_part,
        ]
    )
    return (jnp.stack([residual_real, residual_imag]), weighted, row_weights, column_weights)


def local(
    model_strip,
    screen_angle,
    facet_window,
    facet_shift,
    kernel_taps,
    plane_angle,
    u_cell,
    v_cell,
    w_plane,
    observed,
):
    strip_data = lax.all_gather(model_strip, "layer", axis=3, tiled=True)[0]
    phases = screen_angle[0, 0].astype(jnp.float32)
    cosine = jnp.cos(phases)
    sine_part = jnp.sin(phases)
    strip_values = strip_data.astype(jnp.float32)
    screened = jnp.stack(
        [
            strip_values[0] * cosine - strip_values[1] * sine_part,
            strip_values[0] * sine_part + strip_values[1] * cosine,
        ]
    ).astype(jnp.bfloat16)
    contrib = forward(screened, facet_window[0], facet_shift[0])
    received = lax.all_to_all(contrib, "facet", split_axis=0, concat_axis=0, tiled=True)
    owner_count = lax.axis_size("facet")
    per_owner = received.shape[0] // owner_count
    grids = jnp.sum(
        received.reshape(owner_count, per_owner, SUB_ROWS, 2 * STRIP_COLS).astype(jnp.float32),
        axis=0,
    )
    residual_vis, weighted, row_weights, column_weights = jax.vmap(
        degrid, in_axes=(0, 0, 0, 0, 0, None, None)
    )(grids, u_cell[0], v_cell[0], w_plane[0], observed[0], plane_angle[0], kernel_taps)
    adjoint = jax.vmap(adjoint_from)(row_weights, column_weights, weighted).astype(jnp.bfloat16)
    all_grids = lax.all_gather(adjoint, "facet", axis=0, tiled=True)
    term = backward(all_grids, facet_window[0], facet_shift[0], screen_angle[0, 0]).astype(
        jnp.bfloat16
    )
    pieces = lax.all_to_all(term[None], "layer", split_axis=3, concat_axis=0, tiled=True)
    gradient = jnp.sum(pieces.astype(jnp.float32), axis=0)[None]
    return (residual_vis[None], gradient)


def solution(mesh):
    return jax.shard_map(
        local,
        mesh=mesh,
        in_specs=(
            P("facet", None, None, "layer"),
            P("layer", "facet", None, None),
            P("facet", None),
            P("facet"),
            P(),
            P("layer", None),
            P("layer", "facet", None),
            P("layer", "facet", None),
            P("layer", "facet", None),
            P("layer", "facet", None, None),
        ),
        out_specs=(P("layer", "facet", None, None), P("facet", None, None, "layer")),
        check_vma=False,
    )
```

profile of v0, /device:TPU:0, one launch (start us, length us, event | category | flops | bytes accessed | tf_op | source)
XLA Modules:
  0.0 259.3 jit_solution(13630020163129976060)
XLA Ops:
  7.2 0.0 all-gather.3.cloned.1.call-start
  7.2 0.7 all-gather.3.cloned.1.call-update
  7.9 0.5 broadcast.531
  8.4 1.5 reduce.6
  9.9 0.1 squeeze.12
  10.0 0.1 copy.94
  10.7 1.5 copy.124
  12.2 0.1 sine_negate_fusion.2
  12.3 0.1 sine_negate_fusion.1
  12.5 0.3 sine_negate_fusion
  12.8 0.2 cosine_multiply_fusion
  12.9 0.0 copy-start.2
  13.0 45.0 %all-gather.3.cloned.1.call-done = bf16[1,2,64,8192]{3,2,1,0:T(8,128)(2,1)} async-done(((bf16[1,2,64,2048]{3,2,1,0:T(8,128)(2,1)}), bf16[1,2,64,8192]{3,2,1,0:T(8,128)(2,1)}) %all-gather.3.cloned.1.call-update) | async-done | bytes 2097168 | tf_op jit(solution)/shard_map/all_gather | solution.py:155
  58.0 2.0 convert_element_type.143
  60.0 8.0 %fusion.51 = (bf16[8,8,64,128]{3,1,2,0:T(8,128)(2,1)S(1)}, bf16[8,8,64,128]{3,1,2,0:T(8,128)(2,1)S(1)}) fusion(f32[1,2,64,8192]{3,2,1,0:T(8,128)S(1)} %convert_element_type.143, bf16[1,1,64,8192]{3,2,1,0:T(8,128)(2,1)S(1)} %copy-done.2), kind=kLoop, calls=%fused_computation.93 | loop fusion | flops 4718592 | bytes 7340032
  68.0 0.3 copy.121
  68.2 0.3 copy.122
  68.5 1.2 convolution_bitcast_fusion.1
  69.7 1.1 subtract_convert_fusion.3
  70.9 1.2 convolution_bitcast_fusion.3
  72.1 1.1 subtract_convert_fusion.2
  73.2 0.2 pad_maximum_fusion
  73.4 3.4 %copy.96 = bf16[128,64,128]{2,1,0:T(8,128)(2,1)} copy(bf16[128,64,128]{0,1,2:T(8,128)(2,1)S(1)} %pad_maximum_fusion) | data formatting | bytes 4194304 | tf_op jit(solution)/shard_map/concatenate | solution.py:60
  76.8 4.5 %all-to-all-start = ((bf16[128,64,128]{2,1,0:T(8,128)(2,1)}), bf16[128,64,128]{2,1,0:T(8,128)(2,1)}, u32[]{:S(2)}, u32[]{:S(2)}) async-start(bf16[128,64,128]{2,1,0:T(8,128)(2,1)} %copy.96), calls=%async_computation | async-start | bytes 4194304 | tf_op jit(solution)/shard_map/all_to_all | solution.py:167
  81.3 0.2 all-gather.5.cloned.1.call-start
  81.6 0.0 copy-start.11
  81.6 1.6 add_select_fusion
  83.2 0.0 copy-done.11
  83.3 4.7 %select_reduce_fusion.1 = (f32[16,512,64]{1,2,0:T(8,128)}, f32[16,512,64]{1,2,0:T(8,128)S(1)}) fusion(f32[7]{0:T(128)S(1)} %copy-done.11, s32[16,512,64]{1,2,0:T(8,128)S(1)} %get-tuple-element.38, s32[7]{0:T(128)S(1)} %and_select_fusion, s32[16,512,64]{1,2,0:T(8,128)S(1)} %get-tuple-element.37), kind=kLoop, calls=%fused_computation.1 | loop fusion | flops 20971520 | bytes 8388664 | tf_op jit(solution)/shard_map/vmap()/reduce_sum | solution.py:110
  87.9 2.7 %copy.97 = f32[16,512,64]{2,1,0:T(8,128)} copy(f32[16,512,64]{1,2,0:T(8,128)S(1)} %get-tuple-element.11) | data formatting | bytes 4194304 | tf_op jit(solution)/shard_map/vmap()/reduce_sum | solution.py:110
  90.7 0.1 select_reduce_fusion.2
  90.8 0.1 fusion.107
  90.9 17.0 %all-to-all-done = bf16[128,64,128]{2,1,0:T(8,128)(2,1)} async-done(((bf16[128,64,128]{2,1,0:T(8,128)(2,1)}), bf16[128,64,128]{2,1,0:T(8,128)(2,1)}, u32[]{:S(2)}, u32[]{:S(2)}) %all-to-all-start) | async-done | bytes 2097184 | tf_op jit(solution)/shard_map/all_to_all | solution.py:167
  108.0 2.2 convert_reduce_fusion.1
  110.1 0.1 copy-done
  110.2 3.6 %fusion.108 = f32[16,512,128]{1,2,0:T(8,128)S(1)} fusion(f32[16,512,64]{1,2,0:T(8,128)S(1)} %copy-done, f32[16,64,128]{2,1,0:T(8,128)S(1)} %convert_reduce_fusion.1), kind=kOutput, calls=%fused_computation.183 | convolution fusion | flops 805306368 | bytes 6815744 | tf_op jit(solution)/shard_map/vmap()/dot_general | solution.py:123
  113.8 0.0 copy-start.7
  113.8 0.0 copy-start.1
  113.9 0.9 fusion.24
  114.8 0.0 copy-start.5
  114.9 1.2 copy-done.1
  116.1 2.5 broadcast_multiply_fusion.1
  118.6 4.1 %fusion.45 = bf16[16,64,128]{2,1,0:T(8,128)(2,1)} fusion(f32[16,512,64]{1,2,0:T(8,128)S(1)} %copy-done, f32[16,512,64]{2,1,0:T(8,128)S(1)} %get-tuple-element.30, f32[16,512,64]{2,1,0:T(8,128)S(1)} %get-tuple-element.29), kind=kOutput, calls=%fused_computation.89 | convolution fusion | flops 806486016 | bytes 6553600 | tf_op jit(solution)/shard_map/vmap()/dot_general | solution.py:117
  122.6 0.0 all-gather.5.cloned.1.call-update
  122.6 25.1 %all-gather.5.cloned.1.call-done = bf16[128,64,128]{2,1,0:T(8,128)(2,1)} async-done(((bf16[16,64,128]{2,1,0:T(8,128)(2,1)}), bf16[128,64,128]{2,1,0:T(8,128)(2,1)}) %all-gather.5.cloned.1.call-update) | async-done | bytes 2097168 | tf_op jit(solution)/shard_map/all_gather | solution.py:178
  147.8 4.1 %copy.99 = bf16[128,64,128]{0,1,2:T(8,128)(2,1)S(1)} copy(bf16[128,64,128]{2,1,0:T(8,128)(2,1)} %all-gather.5.cloned.1.call-done) | data formatting | bytes 4194304 | tf_op jit(solution)/shard_map/all_gather | solution.py:178
  151.9 0.4 convert_element_type.154
  152.3 0.6 fusion.48
  152.9 1.2 convolution_bitcast_fusion.2
  154.2 1.1 add_convert_fusion
  155.3 1.3 convolution_bitcast_fusion
  156.6 2.9 %slice_subtract_fusion = (f32[1,1,64,64,128]{4,3,0,2,1:T(8,128)}, f32[1,1,64,64,128]{4,3,0,2,1:T(8,128)}) fusion(f32[2,2,64,64,128]{4,3,0,2,1:T(8,128)S(1)} %convolution_bitcast_fusion), kind=kLoop, calls=%fused_computation.38 | loop fusion | flops 1048576 | bytes 12582912 | tf_op jit(solution)/shard_map/sub | solution.py:96
  159.5 1.7 add.275
  161.2 2.8 %sub.229 = f32[1,1,64,8192]{3,2,1,0:T(8,128)} reshape(f32[1,1,64,64,128]{4,3,0,2,1:T(8,128)} %get-tuple-element.21) | data formatting | bytes 4194304 | tf_op jit(solution)/shard_map/sub | solution.py:96
  164.0 8.8 %fusion.17 = (f32[1,1,64,8192]{3,2,1,0:T(8,128)S(1)}, f32[1,1,64,8192]{3,2,1,0:T(8,128)S(1)}) fusion(f32[1,1,64,8192]{3,2,1,0:T(8,128)} %sub.229, bf16[1,1,64,8192]{3,2,1,0:T(8,128)(2,1)S(1)} %copy-done.2, f32[1,1,64,8192]{3,2,1,0:T(8,128)S(1)} %add.275), kind=kLoop, calls=%fused_computation.34 | loop fusion | flops 3670016 | bytes 9437184 | tf_op jit(solution)/shard_map/add | solution.py:101
  172.8 0.3 fusion.4
  173.0 6.8 %copy.103 = bf16[1,2,64,8192]{2,1,0,3:T(2,128)(2,1)} copy(bf16[1,2,64,8192]{3,2,1,0:T(8,128)(2,1)S(1)} %fusion.4) | data formatting | bytes 4194304 | tf_op jit(solution)/shard_map/convert_element_type | solution.py:179
  179.9 5.9 %reshape.702 = bf16[4,2,131072]{2,1,0:T(2,128)(2,1)} reshape(bf16[8192,1,2,64]{3,2,1,0:T(2,128)(2,1)} %bitcast.221) | data formatting | bytes 4194304
  185.8 4.7 %all-to-all-start.1 = ((bf16[4,2,131072]{2,1,0:T(2,128)(2,1)}), bf16[4,2,131072]{2,1,0:T(2,128)(2,1)S(1)}, u32[]{:S(2)}, u32[]{:S(2)}) async-start(bf16[4,2,131072]{2,1,0:T(2,128)(2,1)} %reshape.702), calls=%async_computation.1 | async-start | bytes 4194304 | tf_op jit(solution)/shard_map/all_to_all | solution.py:182
  190.5 0.7 copy.104
  191.2 47.9 %all-to-all-done.1 = bf16[4,2,131072]{2,1,0:T(2,128)(2,1)S(1)} async-done(((bf16[4,2,131072]{2,1,0:T(2,128)(2,1)}), bf16[4,2,131072]{2,1,0:T(2,128)(2,1)S(1)}, u32[]{:S(2)}, u32[]{:S(2)}) %all-to-all-start.1) | async-done | bytes 2097184 | tf_op jit(solution)/shard_map/all_to_all | solution.py:182
  239.1 4.0 %reshape.703 = bf16[8192,1,2,64]{3,2,1,0:T(2,128)(2,1)} reshape(bf16[4,2,131072]{2,1,0:T(2,128)(2,1)S(1)} %all-to-all-done.1) | data formatting | bytes 4194304
  243.1 7.3 %convert_reduce_fusion = f32[2,64,2048]{1,0,2:T(2,128)S(1)} fusion(bf16[2,64,4,2048]{1,0,3,2:T(2,128)(2,1)} %bitcast.222), kind=kLoop, calls=%fused_computation.2 | loop fusion | flops 1835008 | bytes 3145728 | tf_op jit(solution)/shard_map/reduce_sum | solution.py:183
  250.4 2.1 copy.105
  (24 shorter events, 0.1 us)
Async XLA Ops:
  7.2 50.8 %all-gather.3.cloned.1.call-start = ((), (), s32[]{:S(2)}) async-start(), calls=%async_computation.2 | async-start | bytes 2621440 | tf_op jit(solution)/shard_map/all_gather | solution.py:155
  12.9 47.0 %copy-start.2 = (bf16[1,1,64,8192]{3,2,1,0:T(8,128)(2,1)S(1)}, bf16[1,1,64,8192]{3,2,1,0:T(8,128)(2,1)}, u32[]{:S(2)}) copy-start(bf16[1,1,64,8192]{3,2,1,0:T(8,128)(2,1)} %param.11) | copy-start | bytes 3145732
  76.8 4.7 %copy-start.8 = (s32[1,16,512]{2,1,0:T(8,128)S(1)}, s32[1,16,512]{2,1,0:T(8,128)}, u32[]{:S(2)}) copy-start(s32[1,16,512]{2,1,0:T(8,128)} %param.17) | copy-start | bytes 98308
  76.8 4.8 %copy-start.9 = (s32[1,16,512]{2,1,0:T(8,128)S(1)}, s32[1,16,512]{2,1,0:T(8,128)}, u32[]{:S(2)}) copy-start(s32[1,16,512]{2,1,0:T(8,128)} %param.16) | copy-start | bytes 98308
  76.8 31.1 %all-to-all-start = ((bf16[128,64,128]{2,1,0:T(8,128)(2,1)}), bf16[128,64,128]{2,1,0:T(8,128)(2,1)}, u32[]{:S(2)}, u32[]{:S(2)}) async-start(bf16[128,64,128]{2,1,0:T(8,128)(2,1)} %copy.96), calls=%async_computation | async-start | bytes 4194304 | tf_op jit(solution)/shard_map/all_to_all | solution.py:167
  81.3 66.4 %all-gather.5.cloned.1.call-start = ((), (), s32[]{:S(2)}) async-start(), calls=%async_computation.3 | async-start | bytes 2359296 | tf_op jit(solution)/shard_map/all_gather | solution.py:178
  81.6 1.6 copy-start.11
  87.9 2.7 %copy-start.10 = (s32[1,16,512]{2,1,0:T(8,128)S(1)}, s32[1,16,512]{2,1,0:T(8,128)}, u32[]{:S(2)}) copy-start(s32[1,16,512]{2,1,0:T(8,128)} %param.18) | copy-start | bytes 98308
  87.9 2.7 %copy-start.12 = (f32[1,8]{1,0:T(1,128)S(1)}, f32[1,8]{1,0:T(1,128)}, u32[]{:S(2)}) copy-start(f32[1,8]{1,0:T(1,128)} %param.15) | copy-start | bytes 100
  108.0 2.2 copy-start
  113.8 0.9 copy-start.7
  113.8 2.2 copy-start.1
  114.8 3.7 %copy-start.3 = (f32[1,16,512]{2,1,0:T(8,128)}, f32[1,16,512]{2,1,0:T(8,128)S(1)}, u32[]{:S(2)}) copy-start(f32[1,16,512]{2,1,0:T(8,128)S(1)} %get-tuple-element.13) | copy-start | bytes 98308
  114.8 3.7 %copy-start.5 = (f32[1,16,512]{2,1,0:T(8,128)}, f32[1,16,512]{2,1,0:T(8,128)S(1)}, u32[]{:S(2)}) copy-start(f32[1,16,512]{2,1,0:T(8,128)S(1)} %get-tuple-element.14) | copy-start | bytes 98308
  185.8 4.7 %copy-start.4 = (f32[1,16,512]{2,1,0:T(8,128)S(1)}, f32[1,16,512]{2,1,0:T(8,128)}, u32[]{:S(2)}) copy-start(f32[1,16,512]{2,1,0:T(8,128)} %copy-done.3) | copy-start | bytes 98308
  185.8 4.7 %copy-start.6 = (f32[1,16,512]{2,1,0:T(8,128)S(1)}, f32[1,16,512]{2,1,0:T(8,128)}, u32[]{:S(2)}) copy-start(f32[1,16,512]{2,1,0:T(8,128)} %copy-done.5) | copy-start | bytes 98308
  185.8 53.3 %all-to-all-start.1 = ((bf16[4,2,131072]{2,1,0:T(2,128)(2,1)}), bf16[4,2,131072]{2,1,0:T(2,128)(2,1)S(1)}, u32[]{:S(2)}, u32[]{:S(2)}) async-start(bf16[4,2,131072]{2,1,0:T(2,128)(2,1)} %reshape.702), calls=%async_computation.1 | async-start | bytes 4194304 | tf_op jit(solution)/shard_map/all_to_all | solution.py:182
Sparse Core Ops, SparseCore 0:
  9.5 48.3 all-gather.2
  122.8 24.9 all-gather.4
where the time goes:
time: 260 us; the launch traced here: 259 us
  waiting for transfers between devices  136 us (52%)
  other arithmetic  47.9 us (18%)
  local copies, waits for them, and re-layouts  38.4 us (15%)
  between operations  15.1 us (6%)
  matrix products  12.7 us (5%)
  starting transfers between devices  9.47 us (4%)
    all_to_all x1, waiting for transfers between devices, local(): lax.all_to_all(term[None], 'layer', split_axis=3, concat_axis=0, tiled=True)  47.9 us
    all_gather x1, waiting for transfers between devices, local(): strip_data = lax.all_gather(model_strip, 'layer', axis=3, tiled=True)[0]  45 us
    all_gather x1, waiting for transfers between devices, local(): all_grids = lax.all_gather(adjoint, 'facet', axis=0, tiled=True)  25.1 us
    all_to_all x1, waiting for transfers between devices, local(): lax.all_to_all(contrib, 'facet', split_axis=0, concat_axis=0, tiled=True)  17 us
    unnamed x34, local copies, waits for them, and re-layouts  16.6 us
    unnamed x2, other arithmetic  9.45 us
    add x1, other arithmetic, backward(): image_real * cosine + image_imag * sine_part  8.78 us
    reduce_sum x1, other arithmetic, local(): gradient = jnp.sum(pieces.astype(jnp.float32), axis=0)[None]  7.26 us
  transfers between devices with their start and end apart: 4, of which 4 were waited for; matrix products, arithmetic and copies ran while one was open for 6% of the time, Pallas kernels for 0%

commit v1 on v0

--- a/solution.py
+++ b/solution.py
@@ -179,7 +179,10 @@
     term = backward(all_grids, facet_window[0], facet_shift[0], screen_angle[0, 0]).astype(
         jnp.bfloat16
     )
-    pieces = lax.all_to_all(term[None], "layer", split_axis=3, concat_axis=0, tiled=True)
+    part = term[None]
+    shards = jnp.split(part, lax.axis_size("layer"), axis=3)
+    got = lax.all_to_all(jnp.stack(shards), "layer", 0, 0)
+    pieces = jnp.concatenate(got, axis=0)
     gradient = jnp.sum(pieces.astype(jnp.float32), axis=0)[None]
     return (residual_vis[None], gradient)
 

time: 260 us -> 237 us (0.912)
  local copies, waits for them, and re-layouts: 38.4 us -> 19.7 us
  other arithmetic: 47.9 us -> 43.6 us
    unnamed x34 -> x31, local copies, waits for them, and re-layouts: 16.6 us -> 4.54 us
    convert_element_type x1 -> x0, local copies, waits for them, and re-layouts: 6.85 us -> none  [local(): backward(all_grids, facet_window[0], facet_shift[0], screen_angle[0, 0])]
    reduce_sum x1, other arithmetic: 7.26 us -> 1.35 us  [local(): gradient = jnp.sum(pieces.astype(jnp.float32), axis=0)[None]]
where the time goes in v1:
time: 237 us; the launch traced here: 236 us
  waiting for transfers between devices  136 us (57%)
  other arithmetic  43.6 us (18%)
  local copies, waits for them, and re-layouts  19.7 us (8%)
  between operations  15.1 us (6%)
  matrix products  12.7 us (5%)
  starting transfers between devices  9.47 us (4%)
    all_to_all x1, waiting for transfers between devices, local(): got = lax.all_to_all(jnp.stack(shards), 'layer', 0, 0)  47.9 us
    all_gather x1, waiting for transfers between devices, local(): strip_data = lax.all_gather(model_strip, 'layer', axis=3, tiled=True)[0]  45 us
    all_gather x1, waiting for transfers between devices, local(): all_grids = lax.all_gather(adjoint, 'facet', axis=0, tiled=True)  25.1 us
    all_to_all x1, waiting for transfers between devices, local(): lax.all_to_all(contrib, 'facet', split_axis=0, concat_axis=0, tiled=True)  17 us
    unnamed x2, other arithmetic  9.45 us
    add x1, other arithmetic, backward(): image_real * cosine + image_imag * sine_part  8.78 us
  transfers between devices with their start and end apart: 4, of which 4 were waited for; matrix products, arithmetic and copies ran while one was open for 6% of the time, Pallas kernels for 0%

profile of v1, /device:TPU:0, one launch (start us, length us, event | category | flops | bytes accessed | tf_op | source)
XLA Modules:
  0.0 236.3 jit_solution(4633682786150660480)
XLA Ops:
  7.2 0.0 all-gather.3.cloned.1.call-start
  7.2 0.7 all-gather.3.cloned.1.call-update
  7.9 0.5 broadcast.531
  8.4 1.5 reduce.4
  9.9 0.1 squeeze.12
  10.0 0.1 copy.80
  10.7 1.5 copy.108
  12.2 0.1 sine_negate_fusion.2
  12.3 0.1 sine_negate_fusion.1
  12.5 0.3 sine_negate_fusion
  12.8 0.2 cosine_multiply_fusion
  12.9 0.0 copy-start.2
  13.0 45.0 %all-gather.3.cloned.1.call-done = bf16[1,2,64,8192]{3,2,1,0:T(8,128)(2,1)} async-done(((bf16[1,2,64,2048]{3,2,1,0:T(8,128)(2,1)}), bf16[1,2,64,8192]{3,2,1,0:T(8,128)(2,1)}) %all-gather.3.cloned.1.call-update) | async-done | bytes 2097168 | tf_op jit(solution)/shard_map/all_gather | solution.py:155
  58.0 2.0 convert_element_type.139
  60.0 8.0 %fusion.51 = (bf16[8,8,64,128]{3,1,2,0:T(8,128)(2,1)S(1)}, bf16[8,8,64,128]{3,1,2,0:T(8,128)(2,1)S(1)}) fusion(f32[1,2,64,8192]{3,2,1,0:T(8,128)S(1)} %convert_element_type.139, bf16[1,1,64,8192]{3,2,1,0:T(8,128)(2,1)S(1)} %copy-done.2), kind=kLoop, calls=%fused_computation.94 | loop fusion | flops 4718592 | bytes 7340032
  68.0 0.3 copy.105
  68.2 0.3 copy.106
  68.5 1.2 convolution_bitcast_fusion.1
  69.7 1.1 subtract_convert_fusion.3
  70.9 1.2 convolution_bitcast_fusion.3
  72.1 1.1 subtract_convert_fusion.2
  73.2 0.2 pad_maximum_fusion
  73.4 3.4 %copy.82 = bf16[128,64,128]{2,1,0:T(8,128)(2,1)} copy(bf16[128,64,128]{0,1,2:T(8,128)(2,1)S(1)} %pad_maximum_fusion) | data formatting | bytes 4194304 | tf_op jit(solution)/shard_map/concatenate | solution.py:60
  76.8 4.5 %all-to-all-start = ((bf16[128,64,128]{2,1,0:T(8,128)(2,1)}), bf16[128,64,128]{2,1,0:T(8,128)(2,1)}, u32[]{:S(2)}, u32[]{:S(2)}) async-start(bf16[128,64,128]{2,1,0:T(8,128)(2,1)} %copy.82), calls=%async_computation | async-start | bytes 4194304 | tf_op jit(solution)/shard_map/all_to_all | solution.py:167
  81.3 0.2 all-gather.5.cloned.1.call-start
  81.6 0.0 copy-start.11
  81.6 1.6 add_select_fusion
  83.2 0.0 copy-done.11
  83.2 4.7 %select_reduce_fusion.1 = (f32[16,512,64]{1,2,0:T(8,128)}, f32[16,512,64]{1,2,0:T(8,128)S(1)}) fusion(f32[7]{0:T(128)S(1)} %copy-done.11, s32[16,512,64]{1,2,0:T(8,128)S(1)} %get-tuple-element.40, s32[7]{0:T(128)S(1)} %and_select_fusion, s32[16,512,64]{1,2,0:T(8,128)S(1)} %get-tuple-element.39), kind=kLoop, calls=%fused_computation.1 | loop fusion | flops 20971520 | bytes 8388664 | tf_op jit(solution)/shard_map/vmap()/reduce_sum | solution.py:110
  87.9 2.7 %copy.83 = f32[16,512,64]{2,1,0:T(8,128)} copy(f32[16,512,64]{1,2,0:T(8,128)S(1)} %get-tuple-element.9) | data formatting | bytes 4194304 | tf_op jit(solution)/shard_map/vmap()/reduce_sum | solution.py:110
  90.7 0.1 select_reduce_fusion.2
  90.8 0.1 fusion.107
  90.9 17.0 %all-to-all-done = bf16[128,64,128]{2,1,0:T(8,128)(2,1)} async-done(((bf16[128,64,128]{2,1,0:T(8,128)(2,1)}), bf16[128,64,128]{2,1,0:T(8,128)(2,1)}, u32[]{:S(2)}, u32[]{:S(2)}) %all-to-all-start) | async-done | bytes 2097184 | tf_op jit(solution)/shard_map/all_to_all | solution.py:167
  108.0 2.2 convert_reduce_fusion
  110.1 0.1 copy-done
  110.2 3.6 %fusion.108 = f32[16,512,128]{1,2,0:T(8,128)S(1)} fusion(f32[16,512,64]{1,2,0:T(8,128)S(1)} %copy-done, f32[16,64,128]{2,1,0:T(8,128)S(1)} %convert_reduce_fusion), kind=kOutput, calls=%fused_computation.188 | convolution fusion | flops 805306368 | bytes 6815744 | tf_op jit(solution)/shard_map/vmap()/dot_general | solution.py:123
  113.8 0.0 copy-start.7
  113.8 0.0 copy-start.1
  113.8 0.9 fusion.24
  114.8 0.0 copy-done.7
  114.8 0.0 copy-start.5
  114.9 1.2 copy-done.1
  116.1 2.5 %broadcast_multiply_fusion.1 = (f32[16,512,64]{2,1,0:T(8,128)S(1)}, f32[16,512,64]{2,1,0:T(8,128)S(1)}) fusion(f32[16,512,64]{2,1,0:T(8,128)S(1)} %copy-done.1, f32[16,512]{1,0:T(8,128)S(1)} %get-tuple-element.33, f32[16,512]{1,0:T(8,128)S(1)} %get-tuple-element.34), kind=kLoop, calls=%fused_computation.79 | loop fusion | flops 1048576 | bytes 6356992 | tf_op jit(solution)/shard_map/vmap()/mul | solution.py:115
  118.5 0.0 copy-done.3
  118.6 4.1 %fusion.45 = bf16[16,64,128]{2,1,0:T(8,128)(2,1)} fusion(f32[16,512,64]{1,2,0:T(8,128)S(1)} %copy-done, f32[16,512,64]{2,1,0:T(8,128)S(1)} %get-tuple-element.28, f32[16,512,64]{2,1,0:T(8,128)S(1)} %get-tuple-element.27), kind=kOutput, calls=%fused_computation.90 | convolution fusion | flops 806486016 | bytes 6553600 | tf_op jit(solution)/shard_map/vmap()/dot_general | solution.py:117
  122.6 0.0 all-gather.5.cloned.1.call-update
  122.6 25.1 %all-gather.5.cloned.1.call-done = bf16[128,64,128]{2,1,0:T(8,128)(2,1)} async-done(((bf16[16,64,128]{2,1,0:T(8,128)(2,1)}), bf16[128,64,128]{2,1,0:T(8,128)(2,1)}) %all-gather.5.cloned.1.call-update) | async-done | bytes 2097168 | tf_op jit(solution)/shard_map/all_gather | solution.py:178
  147.8 4.1 %copy.85 = bf16[128,64,128]{0,1,2:T(8,128)(2,1)S(1)} copy(bf16[128,64,128]{2,1,0:T(8,128)(2,1)} %all-gather.5.cloned.1.call-done) | data formatting | bytes 4194304 | tf_op jit(solution)/shard_map/all_gather | solution.py:178
  151.9 0.4 convert_element_type.150
  152.3 0.6 fusion.48
  152.9 1.2 convolution_bitcast_fusion.2
  154.2 1.1 add_convert_fusion
  155.3 1.3 convolution_bitcast_fusion
  156.6 2.9 %slice_subtract_fusion = (f32[1,1,64,64,128]{4,3,0,2,1:T(8,128)}, f32[1,1,64,64,128]{4,3,0,2,1:T(8,128)}) fusion(f32[2,2,64,64,128]{4,3,0,2,1:T(8,128)S(1)} %convolution_bitcast_fusion), kind=kLoop, calls=%fused_computation.38 | loop fusion | flops 1048576 | bytes 12582912 | tf_op jit(solution)/shard_map/sub | solution.py:96
  159.5 1.7 add.275
  161.2 2.7 %sub.229 = f32[1,1,64,8192]{3,2,1,0:T(8,128)} reshape(f32[1,1,64,64,128]{4,3,0,2,1:T(8,128)} %get-tuple-element.19) | data formatting | bytes 4194304 | tf_op jit(solution)/shard_map/sub | solution.py:96
  164.0 8.8 %fusion.17 = (f32[1,1,64,8192]{3,2,1,0:T(8,128)S(1)}, f32[1,1,64,8192]{3,2,1,0:T(8,128)S(1)}) fusion(f32[1,1,64,8192]{3,2,1,0:T(8,128)} %sub.229, bf16[1,1,64,8192]{3,2,1,0:T(8,128)(2,1)S(1)} %copy-done.2, f32[1,1,64,8192]{3,2,1,0:T(8,128)S(1)} %add.275), kind=kLoop, calls=%fused_computation.34 | loop fusion | flops 3670016 | bytes 9437184 | tf_op jit(solution)/shard_map/add | solution.py:101
  172.7 0.3 fusion.4
  173.0 0.1 slice_bitcast_fusion.7
  173.2 1.6 pad_maximum_fusion.1
  174.8 4.7 %all-to-all-start.1 = ((bf16[4,1,2,64,2048]{4,3,2,1,0:T(8,128)(2,1)}), bf16[4,1,2,64,2048]{4,3,2,1,0:T(8,128)(2,1)S(1)}, u32[]{:S(2)}, u32[]{:S(2)}) async-start(bf16[4,1,2,64,2048]{4,3,2,1,0:T(8,128)(2,1)} %pad_maximum_fusion.1), calls=%async_computation.1 | async-start | bytes 4194304 | tf_op jit(solution)/shard_map/all_to_all | solution.py:184
  179.5 0.7 copy.89
  180.2 47.9 %all-to-all-done.1 = bf16[4,1,2,64,2048]{4,3,2,1,0:T(8,128)(2,1)S(1)} async-done(((bf16[4,1,2,64,2048]{4,3,2,1,0:T(8,128)(2,1)}), bf16[4,1,2,64,2048]{4,3,2,1,0:T(8,128)(2,1)S(1)}, u32[]{:S(2)}, u32[]{:S(2)}) %all-to-all-start.1) | async-done | bytes 2097184 | tf_op jit(solution)/shard_map/all_to_all | solution.py:184
  228.1 1.3 convert_reduce_fusion.1
  (22 shorter events, 0.1 us)
Async XLA Ops:
  7.2 50.8 %all-gather.3.cloned.1.call-start = ((), (), s32[]{:S(2)}) async-start(), calls=%async_computation.2 | async-start | bytes 2621440 | tf_op jit(solution)/shard_map/all_gather | solution.py:155
  12.9 47.0 %copy-start.2 = (bf16[1,1,64,8192]{3,2,1,0:T(8,128)(2,1)S(1)}, bf16[1,1,64,8192]{3,2,1,0:T(8,128)(2,1)}, u32[]{:S(2)}) copy-start(bf16[1,1,64,8192]{3,2,1,0:T(8,128)(2,1)} %param.11) | copy-start | bytes 3145732
  76.8 4.7 %copy-start.8 = (s32[1,16,512]{2,1,0:T(8,128)S(1)}, s32[1,16,512]{2,1,0:T(8,128)}, u32[]{:S(2)}) copy-start(s32[1,16,512]{2,1,0:T(8,128)} %param.17) | copy-start | bytes 98308
  76.8 4.8 %copy-start.9 = (s32[1,16,512]{2,1,0:T(8,128)S(1)}, s32[1,16,512]{2,1,0:T(8,128)}, u32[]{:S(2)}) copy-start(s32[1,16,512]{2,1,0:T(8,128)} %param.16) | copy-start | bytes 98308
  76.8 31.1 %all-to-all-start = ((bf16[128,64,128]{2,1,0:T(8,128)(2,1)}), bf16[128,64,128]{2,1,0:T(8,128)(2,1)}, u32[]{:S(2)}, u32[]{:S(2)}) async-start(bf16[128,64,128]{2,1,0:T(8,128)(2,1)} %copy.82), calls=%async_computation | async-start | bytes 4194304 | tf_op jit(solution)/shard_map/all_to_all | solution.py:167
  81.3 66.4 %all-gather.5.cloned.1.call-start = ((), (), s32[]{:S(2)}) async-start(), calls=%async_computation.3 | async-start | bytes 2359296 | tf_op jit(solution)/shard_map/all_gather | solution.py:178
  81.6 1.6 copy-start.11
  87.9 2.7 %copy-start.10 = (s32[1,16,512]{2,1,0:T(8,128)S(1)}, s32[1,16,512]{2,1,0:T(8,128)}, u32[]{:S(2)}) copy-start(s32[1,16,512]{2,1,0:T(8,128)} %param.18) | copy-start | bytes 98308
  87.9 2.7 %copy-start.12 = (f32[1,8]{1,0:T(1,128)S(1)}, f32[1,8]{1,0:T(1,128)}, u32[]{:S(2)}) copy-start(f32[1,8]{1,0:T(1,128)} %param.15) | copy-start | bytes 100
  108.0 2.2 copy-start
  113.8 0.9 copy-start.7
  113.8 2.2 copy-start.1
  114.8 3.7 %copy-start.3 = (f32[1,16,512]{2,1,0:T(8,128)}, f32[1,16,512]{2,1,0:T(8,128)S(1)}, u32[]{:S(2)}) copy-start(f32[1,16,512]{2,1,0:T(8,128)S(1)} %get-tuple-element.11) | copy-start | bytes 98308
  114.8 3.7 %copy-start.5 = (f32[1,16,512]{2,1,0:T(8,128)}, f32[1,16,512]{2,1,0:T(8,128)S(1)}, u32[]{:S(2)}) copy-start(f32[1,16,512]{2,1,0:T(8,128)S(1)} %get-tuple-element.12) | copy-start | bytes 98308
  174.8 4.7 %copy-start.4 = (f32[1,16,512]{2,1,0:T(8,128)S(1)}, f32[1,16,512]{2,1,0:T(8,128)}, u32[]{:S(2)}) copy-start(f32[1,16,512]{2,1,0:T(8,128)} %copy-done.3) | copy-start | bytes 98308
  174.8 4.7 %copy-start.6 = (f32[1,16,512]{2,1,0:T(8,128)S(1)}, f32[1,16,512]{2,1,0:T(8,128)}, u32[]{:S(2)}) copy-start(f32[1,16,512]{2,1,0:T(8,128)} %copy-done.5) | copy-start | bytes 98308
  174.8 53.3 %all-to-all-start.1 = ((bf16[4,1,2,64,2048]{4,3,2,1,0:T(8,128)(2,1)}), bf16[4,1,2,64,2048]{4,3,2,1,0:T(8,128)(2,1)S(1)}, u32[]{:S(2)}, u32[]{:S(2)}) async-start(bf16[4,1,2,64,2048]{4,3,2,1,0:T(8,128)(2,1)} %pad_maximum_fusion.1), calls=%async_computation.1 | async-start | bytes 4194304 | tf_op jit(solution)/shard_map/all_to_all | solution.py:184
Sparse Core Ops, SparseCore 0:
  9.5 48.3 all-gather.2
  122.8 24.9 all-gather.4
